TPU v7x, 32 devices: a whole 2x2x4 slice. The times are simulated.
32 devices in a mesh: band: 8 (over z, x), ga: 4 (over y, core).
Axes of the slice: x: 2, y: 2, z: 4, core: 2. Of those that a mesh axis runs over, the one named last changes fastest.
Arguments:
- elements: bfloat16 [2, 768, 2048], P(None, 'band', 'ga'), may hold values from -0.75 to 0.75
- screened: bfloat16 [2, 2, 2048, 2048], P(None, None, 'ga'), may hold values from -0.09375 to 0.09375
- energies: float32 [768], replicated, may hold values from -3 to 3
- freq_points: float32 [2], replicated, may hold values from -3 to 3
- freq_weights: float32 [2], replicated, may hold values from 0.5 to 2
- band_of_slot: int32 [768], replicated, may hold values from 0 to 767, each once
Outputs:
- sigma: float32 [2, 768, 768], P(None, 'band', 'ga')
Inputs may be any that keep to these rules, and one draw needn't show every extreme that they name: `band_of_slot`: each of 0 to 767 stands once.
All inputs are finite; a program needn't handle non-finite values.
Results may differ from a plain program's by a relative error of at most 0.0042.
Values may be sent and summed in bfloat16 or wider, within the bound.
No kernel may reach another device: no remote copies, remote signals or barrier semaphores. Data moves between devices by JAX's collectives and lax.ppermute only.
A program may use at most 128 MiB of HBM per device.

v0:
```python
import jax
import jax.numpy as jnp
from jax import lax
from jax.sharding import PartitionSpec as P


def make_left(block):
    flipped = jnp.stack([-block[1], block[0]])
    return jnp.stack([block, flipped])


def on_device(elements, screened, energies, freq_points, freq_weights, band_of_slot):
    bands = elements.shape[1]
    slot_energy = jnp.take(energies, band_of_slot)
    offset = slot_energy[None, :] - freq_points[:, None]
    screen = freq_weights[:, None] / (1.0 + 4.0 * offset * offset)
    own_start = lax.axis_index("band") * bands
    screen_own = lax.dynamic_slice_in_dim(screen, own_start, bands, 1)
    piece = lax.all_gather(elements, "ga", axis=2, tiled=True)
    real_side = jnp.stack([piece[0], -piece[1]])
    imag_side = jnp.stack([piece[1], piece[0]])
    sides = jnp.stack([real_side, imag_side])
    applied = jnp.einsum(
        "dcmk,wcgk->wdmg", sides, screened, preferred_element_type=jnp.float32
    ).astype(jnp.bfloat16)
    left_own = make_left(elements)
    pairs = jnp.einsum(
        "dcnk,wcmk->wdnm",
        left_own,
        lax.all_gather(applied, "band", axis=2, tiled=True),
        preferred_element_type=jnp.float32,
    )
    factor = 0.5 * (screen_own[:, :, None] + screen[:, None, :])
    partial_rows = jnp.sum(pairs * factor[:, None], axis=0)
    return lax.psum_scatter(partial_rows, "ga", scatter_dimension=2, tiled=True)


def solution(mesh):
    placed = (P(None, "band", "ga"), P(None, None, "ga", None), P(), P(), P(), P())
    return jax.shard_map(
        on_device, mesh=mesh, in_specs=placed, out_specs=P(None, "band", "ga"), check_vma=False
    )
```

profile of v0, /device:TPU:0, one launch (start us, length us, event | category | flops | bytes accessed | tf_op | source)
XLA Modules:
  0.0 121.1 jit_solution(2113868990376874802)
XLA Ops:
  6.5 0.0 copy-start
  6.5 0.0 all-gather.2.cloned.1.call-start
  6.5 10.4 %all_gather.6 = bf16[2,96,2048]{2,1,0:T(8,128)(2,1)S(1)} all-gather(bf16[2,96,512]{2,1,0:T(8,128)(2,1)} %param.6), channel_id=1, replica_groups=mesh['band'=8,'ga'=4] {'ga'}, dimensions={2}, use_global_device_ids=true | all-gather | bytes 983040 | tf_op jit(solution)/shard_map/all_gather | solution.py:19
  17.0 0.1 slice_negate_fusion.1
  17.1 0.1 maximum_bitcast_fusion.8
  17.2 0.0 copy-start.2
  17.2 7.0 %fusion.21 = bf16[2,2,96,512]{3,2,1,0:T(8,128)(2,1)} fusion(bf16[2,2,512,2048]{3,2,1,0:T(8,128)(2,1)} %param.7, bf16[1,2,96,2048]{3,2,1,0:T(8,128)(2,1)S(1)} %get-tuple-element.9, bf16[1,2,96,2048]{3,2,1,0:T(8,128)(2,1)S(1)} %get-tuple-element.8), kind=kOutput, calls=%fused_computation.13 | convolution fusion | flops 1613955072 | bytes 10354688 | tf_op jit(solution)/shard_map/dcmk,wcgk->wdmg/dot_general | solution.py:23
  24.2 0.0 copy-start.3
  24.2 0.0 copy-start.4
  24.2 0.0 copy-start.1
  24.2 0.0 all-gather.2.cloned.1.call-update
  24.3 0.0 reduce-scatter.4.cloned.1.call-start
  24.3 0.0 copy-done.2
  24.4 0.0 copy-done
  24.4 3.2 %gather_fusion = f32[768]{0:T(1024)S(1)} fusion(f32[768]{0:T(1024)S(1)} %copy-done, s32[1024]{0:T(1024)S(1)} %pad_clamp_fusion), kind=kCustom, calls=%fused_computation | custom fusion | bytes 9216 | tf_op jit(solution)/shard_map/jit(_take)/gather | solution.py:14
  27.6 0.0 copy-done.3
  27.6 0.0 copy-done.4
  27.6 0.1 fusion.27
  27.7 0.1 constant_dynamic-slice_fusion
  27.8 0.0 copy-done.1
  27.8 0.1 add_multiply_fusion
  27.9 57.3 %all-gather.2.cloned.1.call-done = bf16[2,2,768,512]{3,2,1,0:T(8,128)(2,1)} async-done(((bf16[2,2,96,512]{3,2,1,0:T(8,128)(2,1)}), bf16[2,2,768,512]{3,2,1,0:T(8,128)(2,1)}) %all-gather.2.cloned.1.call-update) | async-done | bytes 3145744 | tf_op jit(solution)/shard_map/all_gather | solution.py:30
  85.3 3.1 %fusion.12 = f32[2,96,768]{2,1,0:T(8,128)S(1)} fusion(bf16[2,2,768,512]{3,2,1,0:T(8,128)(2,1)} %all-gather.2.cloned.1.call-done, f32[2,96,768]{2,1,0:T(8,128)S(1)} %add_multiply_fusion, bf16[1,2,96,512]{3,2,1,0:T(8,128)(2,1)S(1)} %maximum_bitcast_fusion.12, bf16[1,2,96,512]{3,2,1,0:T(8,128)(2,1)S(1)} %bitcast.63), kind=kOutput, calls=%fused_computation.10 | convolution fusion | flops 605208576 | bytes 4718592 | tf_op jit(solution)/shard_map/dcnk,wcmk->wdnm/dot_general | solution.py:27
  88.4 0.5 copy.11
  88.9 1.4 %reshape.63 = f32[768,192]{1,0:T(8,128)} reshape(f32[768,2,96]{2,1,0:T(2,128)S(1)} %bitcast.61) | data formatting | bytes 1179648
  90.2 0.0 reduce-scatter.4.cloned.1.call-update
  90.3 22.0 %reduce-scatter.4.cloned.1.call-done = f32[192,192]{1,0:T(8,128)} async-done(((f32[768,192]{1,0:T(8,128)}), f32[192,192]{1,0:T(8,128)}) %reduce-scatter.4.cloned.1.call-update) | async-done | bytes 147472
  112.3 1.1 reshape.64
  113.4 0.8 copy.12
  (5 shorter events, 0.1 us)
Async XLA Ops:
  6.5 17.8 %copy-start = (f32[768]{0:T(1024)S(1)}, f32[768]{0:T(1024)}, u32[]{:S(2)}) copy-start(f32[768]{0:T(1024)} %param.8) | copy-start | bytes 9220
  6.5 78.7 %all-gather.2.cloned.1.call-start = ((), (), s32[]{:S(2)}) async-start(), calls=%async_computation.1 | async-start | bytes 3538944 | tf_op jit(solution)/shard_map/all_gather | solution.py:30
  17.2 7.1 %copy-start.2 = (s32[768]{0:T(1024)S(1)}, s32[768]{0:T(1024)}, u32[]{:S(2)}) copy-start(s32[768]{0:T(1024)} %param.11) | copy-start | bytes 9220
  24.2 3.3 %copy-start.3 = (f32[2]{0:T(128)S(1)}, f32[2]{0:T(128)}, u32[]{:S(2)}) copy-start(f32[2]{0:T(128)} %param.10) | copy-start | bytes 28
  24.2 3.4 %copy-start.4 = (f32[2]{0:T(128)S(1)}, f32[2]{0:T(128)}, u32[]{:S(2)}) copy-start(f32[2]{0:T(128)} %param.9) | copy-start | bytes 28
  24.2 3.5 %copy-start.1 = (bf16[2,96,512]{2,1,0:T(8,128)(2,1)S(1)}, bf16[2,96,512]{2,1,0:T(8,128)(2,1)}, u32[]{:S(2)}) copy-start(bf16[2,96,512]{2,1,0:T(8,128)(2,1)} %param.6) | copy-start | bytes 589828
  24.3 88.0 %reduce-scatter.4.cloned.1.call-start = ((), (), s32[]{:S(2)}) async-start(), calls=%async_computation.2 | async-start | bytes 983040
Sparse Core Ops, SparseCore 0:
  24.4 60.8 all-gather.1
  90.4 21.8 reduce-scatter.3
where the time goes:
time: 121 us
  waiting for transfers between devices  79.4 us (66%)
  between operations  13.5 us (11%)
  blocking collectives  10.4 us (9%)
  matrix products  10.2 us (8%)
  local copies, waits for them, and re-layouts  7.04 us (6%)
    all_gather x1, waiting for transfers between devices, on_device(): lax.all_gather(applied, 'band', axis=2, tiled=True)  57.3 us
    unnamed x3, waiting for transfers between devices  22.1 us
    all_gather x1, blocking collectives, on_device(): piece = lax.all_gather(elements, 'ga', axis=2, tiled=True)  10.4 us
    dot_general x1, matrix products, on_device(): jnp.einsum('dcmk,wcgk->wdmg', sides, screened, preferred_element_type=jnp...  7.03 us
    unnamed x14, local copies, waits for them, and re-layouts  3.77 us
    gather x1, local copies, waits for them, and re-layouts, on_device(): slot_energy = jnp.take(energies, band_of_slot)  3.19 us
    dot_general x1, matrix products, on_device(): jnp.einsum('dcnk,wcmk->wdnm', left_own, lax.all_gather(applied, 'band', a...  3.12 us
  transfers between devices with their start and end apart: 2, of which 2 were waited for; matrix products, arithmetic and copies ran while one was open for 3% of the time, Pallas kernels for 0%

commit v1 on v0

--- a/solution.py
+++ b/solution.py
@@ -2,6 +2,11 @@
 import jax.numpy as jnp
 from jax import lax
 from jax.sharding import PartitionSpec as P
+
+
+def swapped_in(shard, axis, dim):
+    sent = jnp.stack([shard] * lax.axis_size(axis))
+    return jnp.concatenate(lax.all_to_all(sent, axis, 0, 0), axis=dim)
 
 
 def make_left(block):
@@ -27,7 +32,7 @@
     pairs = jnp.einsum(
         "dcnk,wcmk->wdnm",
         left_own,
-        lax.all_gather(applied, "band", axis=2, tiled=True),
+        swapped_in(applied, "band", 2),
         preferred_element_type=jnp.float32,
     )
     factor = 0.5 * (screen_own[:, :, None] + screen[:, None, :])

time: 121 us -> 138 us (1.14)
  waiting for transfers between devices: 79.4 us -> 88.7 us
  starting transfers between devices: 0.04 us -> 5.98 us
  local copies, waits for them, and re-layouts: 7.04 us -> 10.1 us
  matrix products: 10.2 us -> 7.46 us
    all_to_all x0 -> x1, waiting for transfers between devices: none -> 66.7 us  [swapped_in(): return jnp.concatenate(lax.all_to_all(sent, axis, 0, 0), axis=dim)]
    all_gather x1 -> x0, waiting for transfers between devices: 57.3 us -> none  [on_device(): lax.all_gather(applied, 'band', axis=2, tiled=True)]
    all_to_all x0 -> x1, starting transfers between devices: none -> 5.94 us  [swapped_in(): return jnp.concatenate(lax.all_to_all(sent, axis, 0, 0), axis=dim)]
    another operation x0 -> x1, local copies, waits for them, and re-layouts: none -> 2 us  [swapped_in(): sent = jnp.stack([shard] * lax.axis_size(axis))]
    dot_general x1, matrix products: 3.12 us -> 1.18 us  [on_device(): jnp.einsum('dcnk,wcmk->wdnm', left_own, swapped_in(applied, 'band', 2), p...]
    unnamed x14 -> x16, local copies, waits for them, and re-layouts: 3.77 us -> 4.58 us
    unnamed x3 -> x2, waiting for transfers between devices: 22.1 us -> 22 us
where the time goes in v1:
time: 138 us
  waiting for transfers between devices  88.7 us (64%)
  between operations  13.6 us (10%)
  blocking collectives  10.4 us (8%)
  local copies, waits for them, and re-layouts  10.1 us (7%)
  matrix products  7.46 us (5%)
  starting transfers between devices  5.98 us (4%)
    all_to_all x1, waiting for transfers between devices, swapped_in(): return jnp.concatenate(lax.all_to_all(sent, axis, 0, 0), axis=dim)  66.7 us
    unnamed x2, waiting for transfers between devices  22 us
    all_gather x1, blocking collectives, on_device(): piece = lax.all_gather(elements, 'ga', axis=2, tiled=True)  10.4 us
    dot_general x1, matrix products, on_device(): jnp.einsum('dcmk,wcgk->wdmg', sides, screened, preferred_element_type=jnp...  6.28 us
    all_to_all x1, starting transfers between devices, swapped_in(): return jnp.concatenate(lax.all_to_all(sent, axis, 0, 0), axis=dim)  5.94 us
    unnamed x16, local copies, waits for them, and re-layouts  4.58 us
    gather x1, local copies, waits for them, and re-layouts, on_device(): slot_energy = jnp.take(energies, band_of_slot)  3.19 us
  transfers between devices with their start and end apart: 2, of which 2 were waited for; matrix products, arithmetic and copies ran while one was open for 3% of the time, Pallas kernels for 0%

profile of v1, /device:TPU:0, one launch (start us, length us, event | category | flops | bytes accessed | tf_op | source)
XLA Modules:
  0.0 137.6 jit_solution(18008367494852614007)
XLA Ops:
  6.5 0.0 copy-start
  6.5 10.4 %all_gather.3 = bf16[2,96,2048]{2,1,0:T(8,128)(2,1)S(1)} all-gather(bf16[2,96,512]{2,1,0:T(8,128)(2,1)} %param.6), channel_id=1, replica_groups=mesh['band'=8,'ga'=4] {'ga'}, dimensions={2}, use_global_device_ids=true | all-gather | bytes 983040 | tf_op jit(solution)/shard_map/all_gather | solution.py:24
  17.0 0.1 slice_negate_fusion.1
  17.0 0.1 maximum_bitcast_fusion.8
  17.2 6.3 %fusion.12 = bf16[2,2,96,512]{3,2,0,1:T(8,128)(2,1)S(1)} fusion(bf16[2,2,512,2048]{3,2,1,0:T(8,128)(2,1)} %param.7, bf16[1,2,96,2048]{3,2,1,0:T(8,128)(2,1)S(1)} %get-tuple-element.9, bf16[1,2,96,2048]{3,2,1,0:T(8,128)(2,1)S(1)} %get-tuple-element.8), kind=kOutput, calls=%fused_computation.11 | convolution fusion | flops 1613955072 | bytes 10354688 | tf_op jit(solution)/shard_map/dcmk,wcgk->wdmg/dot_general | solution.py:28
  23.5 2.0 %stack.45 = bf16[8,2,2,96,512]{4,3,2,1,0:T(8,128)(2,1)} broadcast(bf16[2,2,96,512]{3,2,1,0:T(8,128)(2,1)S(1)} %copy.9), dimensions={1,2,3,4} | broadcast | bytes 3538944 | tf_op jit(solution)/shard_map/stack | solution.py:8
  25.5 0.0 copy-start.3
  25.5 5.9 %all-to-all-start = ((bf16[8,2,2,96,512]{4,3,2,1,0:T(8,128)(2,1)}), bf16[8,2,2,96,512]{4,3,2,1,0:T(8,128)(2,1)S(1)}, u32[]{:S(2)}, u32[]{:S(2)}) async-start(bf16[8,2,2,96,512]{4,3,2,1,0:T(8,128)(2,1)} %stack.45), calls=%async_computation | async-start | bytes 6291456 | tf_op jit(solution)/shard_map/all_to_all | solution.py:9
  31.5 0.0 copy-start.4
  31.5 0.0 copy-start.5
  31.5 0.0 copy-start.1
  31.5 0.0 reduce-scatter.4.cloned.1.call-start
  31.5 0.0 copy-done.3
  31.6 0.0 copy-done
  31.6 3.2 %gather_fusion = f32[768]{0:T(1024)S(1)} fusion(f32[768]{0:T(1024)S(1)} %copy-done, s32[1024]{0:T(1024)S(1)} %pad_clamp_fusion), kind=kCustom, calls=%fused_computation | custom fusion | bytes 9216 | tf_op jit(solution)/shard_map/jit(_take)/gather | solution.py:19
  34.8 0.0 copy-done.4
  34.8 0.0 copy-done.5
  34.8 0.1 fusion.18
  34.9 0.1 constant_dynamic-slice_fusion
  35.0 0.0 copy-done.1
  35.0 0.9 add_multiply_fusion
  36.0 66.7 %all-to-all-done = bf16[8,2,2,96,512]{4,3,2,1,0:T(8,128)(2,1)S(1)} async-done(((bf16[8,2,2,96,512]{4,3,2,1,0:T(8,128)(2,1)}), bf16[8,2,2,96,512]{4,3,2,1,0:T(8,128)(2,1)S(1)}, u32[]{:S(2)}, u32[]{:S(2)}) %all-to-all-start) | async-done | bytes 3145760 | tf_op jit(solution)/shard_map/all_to_all | solution.py:9
  102.7 0.0 copy-start.2
  102.7 0.2 copy.10
  102.9 0.8 copy-done.2
  103.7 1.2 fusion.5
  104.9 0.5 copy.15
  105.4 1.4 reshape.73
  106.8 0.0 reduce-scatter.4.cloned.1.call-update
  106.8 22.0 %reduce-scatter.4.cloned.1.call-done = f32[192,192]{1,0:T(8,128)} async-done(((f32[768,192]{1,0:T(8,128)}), f32[192,192]{1,0:T(8,128)}) %reduce-scatter.4.cloned.1.call-update) | async-done | bytes 147472
  128.8 1.1 reshape.74
  129.9 0.8 copy.16
  (6 shorter events, 0.1 us)
Async XLA Ops:
  6.5 25.0 %copy-start = (f32[768]{0:T(1024)S(1)}, f32[768]{0:T(1024)}, u32[]{:S(2)}) copy-start(f32[768]{0:T(1024)} %param.8) | copy-start | bytes 9220
  25.5 6.0 %copy-start.3 = (s32[768]{0:T(1024)S(1)}, s32[768]{0:T(1024)}, u32[]{:S(2)}) copy-start(s32[768]{0:T(1024)} %param.11) | copy-start | bytes 9220
  25.5 77.2 %all-to-all-start = ((bf16[8,2,2,96,512]{4,3,2,1,0:T(8,128)(2,1)}), bf16[8,2,2,96,512]{4,3,2,1,0:T(8,128)(2,1)S(1)}, u32[]{:S(2)}, u32[]{:S(2)}) async-start(bf16[8,2,2,96,512]{4,3,2,1,0:T(8,128)(2,1)} %stack.45), calls=%async_computation | async-start | bytes 6291456 | tf_op jit(solution)/shard_map/all_to_all | solution.py:9
  31.5 3.3 %copy-start.4 = (f32[2]{0:T(128)S(1)}, f32[2]{0:T(128)}, u32[]{:S(2)}) copy-start(f32[2]{0:T(128)} %param.10) | copy-start | bytes 28
  31.5 3.3 %copy-start.5 = (f32[2]{0:T(128)S(1)}, f32[2]{0:T(128)}, u32[]{:S(2)}) copy-start(f32[2]{0:T(128)} %param.9) | copy-start | bytes 28
  31.5 3.5 %copy-start.1 = (bf16[2,96,512]{2,1,0:T(8,128)(2,1)S(1)}, bf16[2,96,512]{2,1,0:T(8,128)(2,1)}, u32[]{:S(2)}) copy-start(bf16[2,96,512]{2,1,0:T(8,128)(2,1)} %param.6) | copy-start | bytes 589828
  31.5 97.3 %reduce-scatter.4.cloned.1.call-start = ((), (), s32[]{:S(2)}) async-start(), calls=%async_computation.2 | async-start | bytes 983040
  102.7 1.1 copy-start.2
Sparse Core Ops, SparseCore 0:
  106.9 21.8 reduce-scatter.3
